TPU v7x, 128 devices: a whole 4x4x4 slice. The times are simulated.
128 devices in a mesh: op: 16 (over z_lo, y, core), tm: 8 (over x, z_hi).
Axes of the slice: x: 4, y: 4, z: 4 (z_hi: 2, z_lo: 2; z = z_hi * 2 + z_lo), core: 2. Of those that a mesh axis runs over, the one named last changes fastest.
Arguments:
- phi: bfloat16 [256, 64, 2, 128, 128], P('op', 'tm'), may hold values from -6 to 6
- tau_fwd: bfloat16 [2, 64, 2, 128, 128], P(None, 'tm'), may hold values from -0.375 to 0.375
- tau_bwd: bfloat16 [2, 64, 2, 128, 128], P(None, 'tm'), may hold values from -0.375 to 0.375
- src_times: int32 [2], replicated, may hold values from 0 to 63
- partner: int32 [256], replicated, may hold values from 0 to 255, each once
Outputs:
- corr: float32 [256, 2, 64, 2, 256], P('op', None, 'tm')
Inputs may be any that keep to these rules, and one draw needn't show every extreme that they name: partner is a permutation of the operators. `src_times`: source times may repeat.
All inputs are finite; a program needn't handle non-finite values.
Results may differ from a plain program's by a relative error of at most 0.0041.
Values may be sent and summed in bfloat16 or wider, within the bound.
A program may use at most 256 MiB of HBM per device.

v0:
```python
import jax
import jax.numpy as jnp
from jax import lax
from jax.sharding import PartitionSpec as P


def from_root(value, axis, source):
    kept = jnp.where(lax.axis_index(axis) == source, value, 0).astype(value.dtype)
    return lax.psum(kept, axis)


def complex_product(spec, left_re, left_im, right_re, right_im):

    def inner(first, second):
        return jnp.einsum(spec, first, second, preferred_element_type=jnp.float32)

    return (
        inner(left_re, right_re) - inner(left_im, right_im),
        inner(left_re, right_im) + inner(left_im, right_re),
    )


def corr_block(panel, source):
    width = panel.shape[-1]
    sink_re = panel[:, :, :, 0]
    sink_im = panel[:, :, :, 1]
    source_re = source[:, :, 0]
    source_im = source[:, :, 1]

    def inner(first, second):
        return jnp.einsum("jstad,ksad->jstk", first, second, preferred_element_type=jnp.float32)

    real_part = inner(sink_re, source_re) + inner(sink_im, source_im)
    imag_part = inner(sink_im, source_re) - inner(sink_re, source_im)
    return jnp.stack([real_part, imag_part], 3) / width


def body(phi, tau_fwd, tau_bwd, src_times, partner):
    time_local = phi.shape[1]
    sources = tau_fwd.shape[0]
    left_re, left_im = complex_product(
        "stab,jtbc->jstac", tau_fwd[:, :, 0], tau_fwd[:, :, 1], phi[:, :, 0], phi[:, :, 1]
    )
    left_re = left_re.astype(jnp.bfloat16)
    left_im = left_im.astype(jnp.bfloat16)
    sink_re, sink_im = complex_product(
        "jstac,stcd->jstad", left_re, left_im, tau_bwd[:, :, 0], tau_bwd[:, :, 1]
    )
    panel = jnp.stack([sink_re.astype(jnp.bfloat16), sink_im.astype(jnp.bfloat16)], 3)
    fields = []
    for source_index in range(sources):
        when = src_times[source_index]
        local = lax.dynamic_index_in_dim(phi, when % time_local, 1, False)
        fields.append(from_root(local, "tm", when // time_local))
    own_sources = jnp.stack(fields, 1)
    mixed = corr_block(panel, lax.all_gather(own_sources, "op", axis=0, tiled=True))
    return jnp.take(mixed, partner, axis=4)


def solution(mesh):
    in_specs = (
        P("op", "tm", None, None, None),
        P(None, "tm", None, None, None),
        P(None, "tm", None, None, None),
        P(),
        P(),
    )
    out_specs = P("op", None, "tm", None, None)
    return jax.shard_map(body, mesh=mesh, in_specs=in_specs, out_specs=out_specs, check_vma=False)
```

profile of v0, /device:TPU:1, one launch (start us, length us, event | category | flops | bytes accessed | tf_op | source)
XLA Modules:
  0.0 409.4 jit_solution(15826648512579424463)
XLA Ops:
  13.0 1.7 constant_dynamic-slice_fusion.1
  14.7 2.5 copy_select_fusion
  17.4 112.4 %all-reduce.3.cloned.1.call-done = (bf16[16,1,2,128,128]{4,0,3,1,2:T(8,128)(2,1)}, bf16[16,1,2,128,128]{4,0,3,1,2:T(8,128)(2,1)}) async-done(((bf16[16,1,2,128,128]{4,0,3,1,2:T(8,128)(2,1)}, bf16[16,1,2,128,128]{4,0,3,1,2:T(8,128)(2,1)}), (bf16[16,1,2,128,128]{4,0,3,1,2:T(8,128)(2,1)}, bf16[16,1,2,128,128]{4,0,3,1,2:T(8,128)(2,1)})) %all-reduce.3.cloned.1.call-update) | async-done | bytes 2097168 | tf_op jit(solution)/shard_map/psum | solution.py:9
  129.8 3.1 pad_maximum_fusion
  132.9 6.1 %fusion.62 = (bf16[16,8,1,128,128]{4,3,2,1,0:T(8,128)(2,1)}, bf16[16,8,1,128,128]{4,3,2,1,0:T(8,128)(2,1)}) fusion(bf16[16,8,2,128,128]{4,3,2,1,0:T(8,128)(2,1)} %param.5), kind=kLoop, calls=%fused_computation.61 | loop fusion | bytes 16777216 | tf_op jit(solution)/shard_map/slice | solution.py:42
  139.0 6.6 %copy.65 = bf16[16,8,1,128,128]{3,4,0,1,2:T(8,128)(2,1)} copy(bf16[16,8,1,128,128]{4,3,2,1,0:T(8,128)(2,1)} %get-tuple-element.10) | data formatting | bytes 8388608
  145.5 6.7 %copy.63 = bf16[16,8,1,128,128]{3,4,0,1,2:T(8,128)(2,1)} copy(bf16[16,8,1,128,128]{4,3,2,1,0:T(8,128)(2,1)} %get-tuple-element.9) | data formatting | bytes 8388608
  152.4 10.5 %fusion.27 = f32[8,16,128,2,128]{4,2,3,1,0:T(8,128)} fusion(bf16[16,8,1,128,128]{3,4,0,1,2:T(8,128)(2,1)} %copy.65, bf16[2,8,1,128,128]{4,3,2,1,0:T(8,128)(2,1)S(1)} %get-tuple-element.12), kind=kOutput, calls=%fused_computation.30 | convolution fusion | flops 1073741824 | bytes 21495808 | tf_op jit(solution)/shard_map/stab,jtbc->jstac/dot_general | solution.py:15
  162.9 8.8 %fusion.25 = f32[8,16,128,2,128]{4,2,3,1,0:T(8,128)} fusion(bf16[16,8,1,128,128]{3,4,0,1,2:T(8,128)(2,1)S(1)} %copy-done, bf16[2,8,1,128,128]{4,3,2,1,0:T(8,128)(2,1)S(1)} %get-tuple-element.12), kind=kOutput, calls=%fused_computation.28 | convolution fusion | flops 1073741824 | bytes 21495808 | tf_op jit(solution)/shard_map/stab,jtbc->jstac/dot_general | solution.py:15
  171.7 13.1 %fusion.19 = bf16[16,2,8,128,128]{3,4,1,0,2:T(8,128)(2,1)} fusion(f32[8,16,128,2,128]{4,2,3,1,0:T(8,128)} %fusion.27, bf16[16,8,1,128,128]{3,4,0,1,2:T(8,128)(2,1)} %copy.63, bf16[2,8,1,128,128]{4,3,2,1,0:T(8,128)(2,1)S(1)} %get-tuple-element.11), kind=kOutput, calls=%fused_computation.26 | convolution fusion | flops 1082130432 | bytes 29884416 | tf_op jit(solution)/shard_map/stab,jtbc->jstac/dot_general | solution.py:15
  184.8 12.7 %fusion.18 = bf16[16,2,8,128,128]{3,4,1,0,2:T(8,128)(2,1)} fusion(f32[8,16,128,2,128]{4,2,3,1,0:T(8,128)} %fusion.25, bf16[16,8,1,128,128]{3,4,0,1,2:T(8,128)(2,1)} %copy.65, bf16[2,8,1,128,128]{4,3,2,1,0:T(8,128)(2,1)S(1)} %get-tuple-element.11), kind=kOutput, calls=%fused_computation.25 | convolution fusion | flops 1082130432 | bytes 29884416 | tf_op jit(solution)/shard_map/stab,jtbc->jstac/dot_general | solution.py:15
  197.5 12.1 %fusion.8 = f32[2,8,16,128,128]{4,3,2,1,0:T(8,128)} fusion(bf16[16,2,8,128,128]{3,4,1,0,2:T(8,128)(2,1)} %fusion.19, bf16[2,8,2,128,128]{4,3,2,1,0:T(8,128)(2,1)S(1)} %copy-done.1), kind=kOutput, calls=%fused_computation.15 | convolution fusion | flops 1073741824 | bytes 25690112 | tf_op jit(solution)/shard_map/jstac,stcd->jstad/dot_general | solution.py:15
  209.6 12.4 %fusion.6 = f32[2,8,16,128,128]{4,3,2,1,0:T(8,128)} fusion(bf16[16,2,8,128,128]{3,4,1,0,2:T(8,128)(2,1)} %fusion.19, bf16[2,8,2,128,128]{4,3,2,1,0:T(8,128)(2,1)S(1)} %copy-done.1), kind=kOutput, calls=%fused_computation.13 | convolution fusion | flops 1073741824 | bytes 25690112 | tf_op jit(solution)/shard_map/jstac,stcd->jstad/dot_general | solution.py:15
  222.1 13.8 %fusion.4 = bf16[16,2,8,128,128]{4,3,0,2,1:T(8,128)(2,1)} fusion(f32[2,8,16,128,128]{4,3,2,1,0:T(8,128)} %fusion.8, bf16[16,2,8,128,128]{3,4,1,0,2:T(8,128)(2,1)} %fusion.18, bf16[2,8,2,128,128]{4,3,2,1,0:T(8,128)(2,1)S(1)} %copy-done.1), kind=kOutput, calls=%fused_computation.11 | convolution fusion | flops 1082130432 | bytes 34078720 | tf_op jit(solution)/shard_map/jstac,stcd->jstad/dot_general | solution.py:15
  235.8 14.3 %fusion.5 = bf16[16,2,8,128,128]{4,3,0,2,1:T(8,128)(2,1)} fusion(f32[2,8,16,128,128]{4,3,2,1,0:T(8,128)} %fusion.6, bf16[16,2,8,128,128]{3,4,1,0,2:T(8,128)(2,1)} %fusion.18, bf16[2,8,2,128,128]{4,3,2,1,0:T(8,128)(2,1)S(1)} %copy-done.1), kind=kOutput, calls=%fused_computation.12 | convolution fusion | flops 1082130432 | bytes 34078720 | tf_op jit(solution)/shard_map/jstac,stcd->jstad/dot_general | solution.py:15
  250.1 63.4 %all-gather.2.cloned.1.call-done = bf16[256,2,2,128,128]{4,0,3,1,2:T(8,128)(2,1)} async-done(((bf16[16,2,2,128,128]{4,0,3,1,2:T(8,128)(2,1)}), bf16[256,2,2,128,128]{4,0,3,1,2:T(8,128)(2,1)}) %all-gather.2.cloned.1.call-update) | async-done | bytes 33554448 | tf_op jit(solution)/shard_map/all_gather | solution.py:56
  313.5 22.2 %fusion.33 = f32[2,256,16,8]{1,2,3,0:T(8,128)S(1)} fusion(bf16[16,2,8,128,128]{4,3,0,2,1:T(8,128)(2,1)} %fusion.4, bf16[256,2,2,128,128]{4,0,3,1,2:T(8,128)(2,1)} %all-gather.2.cloned.1.call-done), kind=kOutput, calls=%fused_computation.36 | convolution fusion | flops 2147483648 | bytes 25427968 | tf_op jit(solution)/shard_map/jstad,ksad->jstk/dot_general | solution.py:31
  335.7 22.3 %fusion.30 = f32[2,256,16,8]{1,2,3,0:T(8,128)S(1)} fusion(bf16[16,2,8,128,128]{4,3,0,2,1:T(8,128)(2,1)} %fusion.5, bf16[256,2,2,128,128]{4,0,3,1,2:T(8,128)(2,1)} %all-gather.2.cloned.1.call-done), kind=kOutput, calls=%fused_computation.35 | convolution fusion | flops 2147483648 | bytes 25427968 | tf_op jit(solution)/shard_map/jstad,ksad->jstk/dot_general | solution.py:31
  358.0 14.0 %fusion.45 = f32[16,2,8,1,256]{4,0,2,1,3:T(8,128)S(1)} fusion(f32[2,256,16,8]{1,2,3,0:T(8,128)S(1)} %fusion.33, bf16[16,2,8,128,128]{4,3,0,2,1:T(8,128)(2,1)} %fusion.5, bf16[256,2,2,128,128]{4,0,3,1,2:T(8,128)(2,1)} %all-gather.2.cloned.1.call-done), kind=kOutput, calls=%fused_computation.40 | convolution fusion | flops 2147549184 | bytes 25690112 | tf_op jit(solution)/shard_map/jstad,ksad->jstk/dot_general | solution.py:31
  372.1 13.8 %fusion.51 = f32[16,2,8,1,256]{4,0,2,1,3:T(8,128)S(1)} fusion(f32[2,256,16,8]{1,2,3,0:T(8,128)S(1)} %fusion.30, bf16[16,2,8,128,128]{4,3,0,2,1:T(8,128)(2,1)} %fusion.4, bf16[256,2,2,128,128]{4,0,3,1,2:T(8,128)(2,1)} %all-gather.2.cloned.1.call-done), kind=kOutput, calls=%fused_computation.42 | convolution fusion | flops 2147549184 | bytes 25690112 | tf_op jit(solution)/shard_map/jstad,ksad->jstk/dot_general | solution.py:31
  385.9 2.6 copy.39
  388.5 5.2 %gather_fusion = f32[256,16,2,8,2]{1,3,4,2,0:T(8,128)} fusion(f32[16,2,8,2,256]{0,2,4,3,1:T(8,128)} %copy.39, s32[1024]{0:T(1024)S(1)} %pad_clamp_fusion), kind=kCustom, calls=%fused_computation | custom fusion | bytes 1049600 | tf_op jit(solution)/shard_map/jit(_take)/gather | solution.py:57
  393.8 4.0 select_bitcast_fusion
  397.8 4.5 %copy.40 = f32[16,2,8,2,256]{4,3,2,1,0:T(2,128)} copy(f32[16,2,8,2,256]{0,2,3,1,4:T(8,128)} %select_bitcast_fusion) | data formatting | bytes 1048576 | tf_op jit(solution)/shard_map/jit(_take)/select_n | solution.py:57
  (18 shorter events, 1.6 us)
Async XLA Ops:
  6.5 123.3 %all-reduce.3.cloned.1.call-start = ((), (), s32[]{:S(2)}) async-start(), calls=%async_computation.1 | async-start | bytes 4194304 | tf_op jit(solution)/shard_map/psum | solution.py:9
  17.3 296.2 %all-gather.2.cloned.1.call-start = ((), (), s32[]{:S(2)}) async-start(), calls=%async_computation | async-start | bytes 35651584 | tf_op jit(solution)/shard_map/all_gather | solution.py:56
  139.0 13.3 %copy-start.3 = (s32[256]{0:T(256)S(1)}, s32[256]{0:T(256)}, u32[]{:S(2)}) copy-start(s32[256]{0:T(256)} %param.9) | copy-start | bytes 3076
  139.0 13.3 %copy-start.2 = (bf16[2,8,2,128,128]{4,3,2,1,0:T(8,128)(2,1)S(1)}, bf16[2,8,2,128,128]{4,3,2,1,0:T(8,128)(2,1)}, u32[]{:S(2)}) copy-start(bf16[2,8,2,128,128]{4,3,2,1,0:T(8,128)(2,1)} %param.6) | copy-start | bytes 3145732
  152.4 10.5 %copy-start = (bf16[16,8,1,128,128]{3,4,0,1,2:T(8,128)(2,1)S(1)}, bf16[16,8,1,128,128]{3,4,0,1,2:T(8,128)(2,1)}, u32[]{:S(2)}) copy-start(bf16[16,8,1,128,128]{3,4,0,1,2:T(8,128)(2,1)} %copy.63) | copy-start | bytes 12582916
  184.8 12.7 %copy-start.1 = (bf16[2,8,2,128,128]{4,3,2,1,0:T(8,128)(2,1)S(1)}, bf16[2,8,2,128,128]{4,3,2,1,0:T(8,128)(2,1)}, u32[]{:S(2)}) copy-start(bf16[2,8,2,128,128]{4,3,2,1,0:T(8,128)(2,1)} %param.7) | copy-start | bytes 3145732
Sparse Core Ops, SparseCore 0:
  17.4 112.3 all-reduce.2
  133.0 180.4 all-gather.1
where the time goes:
time: 413 us; the launch traced here: 409 us
  waiting for transfers between devices  176 us (43%)
  matrix products  170 us (41%)
  local copies, waits for them, and re-layouts  34.8 us (8%)
  between operations  18.9 us (5%)
  other arithmetic  9.7 us (2%)
    psum x1, waiting for transfers between devices, from_root(): return lax.psum(kept, axis)  112 us
    dot_general x8, matrix products, inner(): return jnp.einsum(spec, first, second, preferred_element_type=jnp.float32)  97.7 us
    dot_general x4, matrix products, inner(): jnp.einsum('jstad,ksad->jstk', first, second, preferred_element_type=jnp....  72.3 us
    all_gather x1, waiting for transfers between devices, body(): lax.all_gather(own_sources, 'op', axis=0, tiled=True)  63.4 us
    unnamed x10, local copies, waits for them, and re-layouts  13.3 us
  transfers between devices with their start and end apart: 2, of which 2 were waited for; matrix products, arithmetic and copies ran while one was open for 29% of the time, Pallas kernels for 0%

commit v1 on v0

v1 whole, which is shorter than its diff:
```python
import functools

import jax
import jax.numpy as jnp
from jax import lax
from jax.experimental import pallas as pl
from jax.experimental.pallas import tpu as pltpu
from jax.sharding import PartitionSpec as P

MESH = pl.DeviceIdType.MESH
F32 = jnp.float32
BF16 = jnp.bfloat16
NSEM = 136
COLORS = ((0, 22, "xyz"), (22, 42, "yzx"), (42, 64, "zxy"))


def nxt(v, step):
    return lax.rem(v + step, 4)


def kernel(src, cand, phi, tauf, taub, partner, out, S, P2, acc, stage, fbuf, fl, wb, rs, comb, dd,
           send_sem, recv_sem, phi_sem):
    op = lax.axis_index("op")
    tm = lax.axis_index("tm")
    core = lax.rem(op, 2)
    zl = op // 8
    zh = lax.rem(tm, 2)
    pos = {"x": tm // 2, "y": lax.rem(op // 2, 4), "z": 2 * zh + zl}

    def device(moved, other_core=False):
        at = dict(pos)
        at.update(moved)
        c = 1 - core if other_core else core
        return ((lax.rem(at["z"], 2) * 4 + at["y"]) * 2 + c, at["x"] * 2 + at["z"] // 2)

    count = [0]
    pending = []

    def send(src_ref, dst_ref, target):
        n = count[0]
        count[0] += 1
        copy = pltpu.make_async_remote_copy(
            src_ref=src_ref, dst_ref=dst_ref, send_sem=send_sem.at[n], recv_sem=recv_sem.at[n],
            device_id=target, device_id_type=MESH)
        copy.start()
        pending.append(copy)
        return copy

    def phi_copy(t):
        slot = lax.rem(t, 2)
        return pltpu.make_async_copy(phi.at[:, t], fbuf.at[slot], phi_sem.at[slot])

    phi_copy(0).start()

    peers = [device({d: nxt(pos[d], k)}) for d in "xyz" for k in (1, 3)]
    peers += [device({"z": nxt(pos["z"], 2)}), device({}, True)]
    barrier = pltpu.get_barrier_semaphore()
    for peer in peers:
        pl.semaphore_signal(barrier, inc=1, device_id=peer, device_id_type=MESH)
    pl.semaphore_wait(barrier, len(peers))

    def sandwich(t, carry):
        slot = lax.rem(t, 2)
        phi_copy(t).wait()

        @pl.when(t < 7)
        def _():
            phi_copy(t + 1).start()

        for s in range(2):
            fr, fi = tauf[s, t, 0], tauf[s, t, 1]
            fl[0:128, 0:128] = fr
            fl[0:128, 128:256] = -fi
            fl[128:256, 0:128] = fi
            fl[128:256, 128:256] = fr
            br, bi = taub[s, t, 0], taub[s, t, 1]
            wb[0:128, 0:128] = br
            wb[0:128, 128:256] = bi
            wb[128:256, 0:128] = -bi
            wb[128:256, 128:256] = br

            def pair(jp, c2):
                two = [fbuf[slot, 2 * jp + q].reshape(256, 128) for q in range(2)]
                a = jnp.dot(fl[...], jnp.concatenate(two, axis=1), preferred_element_type=F32).astype(BF16)
                for q in range(2):
                    left = jnp.concatenate([a[0:128, q * 128:q * 128 + 128], a[128:256, q * 128:q * 128 + 128]], axis=1)
                    prod = jnp.dot(left, wb[...], preferred_element_type=F32)
                    row = pl.multiple_of((2 * jp + q) * 128, 128)
                    stage[0, pl.ds(row, 128), :] = prod[:, 0:128]
                    stage[1, pl.ds(row, 128), :] = prod[:, 128:256]
                return c2

            lax.fori_loop(0, 8, pair, 0)

            def turn(ab, c2):
                for q in range(8):
                    for r in range(2):
                        a = ab * 8 + q
                        rows = stage[r, pl.ds(a, 16, stride=128), :]
                        P2[s, a, r, pl.ds(pl.multiple_of(t * 16, 16), 16), :] = rows.astype(BF16)
                return c2

            lax.fori_loop(0, 16, turn, 0)
        return carry

    own_tm = [src[s] // 8 for s in range(2)]
    own_x = [v // 2 for v in own_tm]
    own_zh = [lax.rem(v, 2) for v in own_tm]
    x = pos["x"]
    xp, xm, x2 = nxt(x, 1), nxt(x, 3), nxt(x, 2)
    plus, minus = device({"x": xp}), device({"x": xm})
    first = [
        send(cand.at[x2, 0], rs.at[0], plus),
        send(cand.at[x2, 1], rs.at[1], minus),
        send(cand.at[xp, 1], rs.at[2], plus),
        send(cand.at[xm, 0], rs.at[3], minus),
    ]
    lax.fori_loop(0, 4, sandwich, 0)
    first[0].wait_recv()
    first[1].wait_recv()
    for s in range(2):
        h = slice(32 * s, 32 * s + 32)
        comb[0, h] = jnp.where(own_x[s] == xm, rs[0, h], cand[xp, 0, h])
        comb[1, h] = jnp.where(own_x[s] == xp, rs[1, h], cand[xm, 1, h])
    second = [send(comb.at[0], rs.at[4], plus), send(comb.at[1], rs.at[5], minus)]
    lax.fori_loop(4, 6, sandwich, 0)
    for copy in first[2:] + second:
        copy.wait_recv()
    for s in range(2):
        h = slice(32 * s, 32 * s + 32)
        dd[0, h] = jnp.where(own_x[s] == x, cand[x, 0, h], jnp.where(own_x[s] == xp, rs[3, h], rs[4, h]))
        dd[1, h] = jnp.where(own_x[s] == x, cand[x, 1, h], jnp.where(own_x[s] == xm, rs[2, h], rs[5, h]))
    across = send(dd.at[1 - zh], rs.at[6], device({"z": nxt(pos["z"], 2)}))
    lax.fori_loop(6, 8, sandwich, 0)
    across.wait_recv()
    for s in range(2):
        h = slice(32 * s, 32 * s + 32)
        S[pos["x"], pos["z"], pos["y"], core, h] = jnp.where(own_zh[s] == zh, dd[zh, h], rs[6, h])

    whole = pl.ds(0, 4)

    def box(where, lo, hi):
        at = [where[d] for d in "xzy"]
        return S.at[at[0], at[1], at[2], pl.ds(core, 1), pl.ds(lo, hi - lo)]

    def one(v):
        return pl.ds(v, 1)

    mate = device({}, True)
    mate_copies = {0: [], 1: [], 2: []}

    def share(color, where, lo, hi):
        ref = box(where, lo, hi)
        mate_copies[color].append(send(ref, ref, mate))

    def ring1(color, d, where):
        lo, hi, _ = COLORS[color]
        w = dict(where)
        w[d] = one(pos[d])
        ref = box(w, lo, hi)
        return [send(ref, ref, device({d: nxt(pos[d], k)})) for k in (1, 3)]

    def ring2(color, d, where):
        lo, hi, _ = COLORS[color]
        mid = (lo + hi) // 2
        w = dict(where)
        w[d] = one(nxt(pos[d], 3))
        a = box(w, lo, mid)
        w[d] = one(nxt(pos[d], 1))
        b = box(w, mid, hi)
        return [send(a, a, device({d: nxt(pos[d], 1)})), send(b, b, device({d: nxt(pos[d], 3)}))]

    def arrived(copies):
        for copy in copies:
            copy.wait_recv()

    three = range(3)
    order = [COLORS[c][2] for c in three]
    base = {d: one(pos[d]) for d in "xyz"}
    p1 = [ring1(c, order[c][0], base) for c in three]
    p1b, p2, p2b = [None] * 3, [None] * 3, [None] * 3
    p3 = [[None] * 4 for _ in three]
    p3b = [[None] * 4 for _ in three]
    for c in three:
        arrived(p1[c])
        p1b[c] = ring2(c, order[c][0], base)
    line = [dict(base) for _ in three]
    for c in three:
        arrived(p1b[c])
        line[c][order[c][0]] = whole
        p2[c] = ring1(c, order[c][1], line[c])
        p3[c][0] = ring1(c, order[c][2], line[c])
        share(c, line[c], COLORS[c][0], COLORS[c][1])

    def group(c, k):
        w = dict(line[c])
        w[order[c][1]] = one(nxt(pos[order[c][1]], (0, 3, 1, 2)[k]))
        return w

    for c in three:
        arrived(p2[c])
        p2b[c] = ring2(c, order[c][1], line[c])
        for k in (1, 2):
            p3[c][k] = ring1(c, order[c][2], group(c, k))
            share(c, group(c, k), COLORS[c][0], COLORS[c][1])
    for c in three:
        arrived(p2b[c])
        p3[c][3] = ring1(c, order[c][2], group(c, 3))
        share(c, group(c, 3), COLORS[c][0], COLORS[c][1])
    for k in range(4):
        for c in three:
            arrived(p3[c][k])
            p3b[c][k] = ring2(c, order[c][2], group(c, k))
            for step in (3, 1):
                w = group(c, k)
                w[order[c][2]] = one(nxt(pos[order[c][2]], step))
                share(c, w, COLORS[c][0], COLORS[c][1])
    for k in range(4):
        for c in three:
            arrived(p3b[c][k])
            w = group(c, k)
            w[order[c][2]] = one(nxt(pos[order[c][2]], 2))
            share(c, w, COLORS[c][0], COLORS[c][1])

    acc[...] = jnp.zeros_like(acc)

    def contract(s, a0, a1):
        def step(p, c2):
            xx = p // 2
            z0 = lax.rem(p, 2) * 2
            left, right = [], []
            for a in range(a0, a1):
                half = [S[xx, pl.ds(z0, 2), :, :, s * 32 + a * 2 + r].reshape(256, 128) for r in range(2)]
                left.append(jnp.concatenate(half, axis=0))
                right.append(P2[s, p * 16 + a].reshape(256, 128))
            acc[s] += lax.dot_general(
                jnp.concatenate(left, axis=1), jnp.concatenate(right, axis=1),
                (((1,), (1,)), ((), ())), preferred_element_type=F32)
            return c2

        lax.fori_loop(0, 8, step, 0)

    parts = {0: ((0, 0, 11),), 1: ((0, 11, 16), (1, 0, 5)), 2: ((1, 5, 16),)}
    for c in three:
        arrived(mate_copies[c])
        for part in parts[c]:
            contract(*part)

    hot = (partner[...] == lax.broadcasted_iota(jnp.int32, (256, 256), 0)).astype(F32)
    for s in range(2):
        q = acc[s]
        real = q[0:256, 0:128] + q[256:512, 128:256]
        imag = q[0:256, 128:256] - q[256:512, 0:128]
        for r, v in enumerate((real, imag)):
            got = lax.dot_general(v, hot, (((0,), (0,)), ((), ())), precision=lax.Precision.HIGHEST,
                                  preferred_element_type=F32)
            out[s, r] = got * (1.0 / 128.0)
    for copy in pending:
        copy.wait_send()


def body(phi, tau_fwd, tau_bwd, src_times, partner):
    picked = jnp.stack([lax.dynamic_index_in_dim(phi, src_times[s] % 8, 1, False) for s in range(2)])
    cand = picked.reshape(2, 16, 2, 4, 2, 16, 128).transpose(3, 4, 0, 5, 2, 1, 6).reshape(4, 2, 64, 16, 128)
    vm = pl.BlockSpec(memory_space=pltpu.VMEM)
    res = pl.pallas_call(
        kernel,
        out_shape=jax.ShapeDtypeStruct((2, 2, 128, 256), F32),
        in_specs=[pl.BlockSpec(memory_space=pltpu.SMEM), vm, pl.BlockSpec(memory_space=pl.ANY), vm, vm, vm],
        out_specs=vm,
        scratch_shapes=[
            pltpu.VMEM((4, 4, 4, 2, 64, 16, 128), BF16),
            pltpu.VMEM((2, 128, 2, 128, 128), BF16),
            pltpu.VMEM((2, 512, 256), F32),
            pltpu.VMEM((2, 2048, 128), F32),
            pltpu.VMEM((2, 16, 2, 128, 128), BF16),
            pltpu.VMEM((256, 256), BF16),
            pltpu.VMEM((256, 256), BF16),
            pltpu.VMEM((7, 64, 16, 128), BF16),
            pltpu.VMEM((2, 64, 16, 128), BF16),
            pltpu.VMEM((2, 64, 16, 128), BF16),
            pltpu.SemaphoreType.DMA((NSEM,)),
            pltpu.SemaphoreType.DMA((NSEM,)),
            pltpu.SemaphoreType.DMA((2,)),
        ],
        compiler_params=pltpu.CompilerParams(collective_id=0, has_side_effects=True, vmem_limit_bytes=67043328),
    )(src_times, cand, phi, tau_fwd, tau_bwd, partner.reshape(1, 256))
    return res.reshape(2, 2, 8, 16, 256).transpose(3, 0, 2, 1, 4)


def solution(mesh):
    in_specs = (
        P("op", "tm", None, None, None),
        P(None, "tm", None, None, None),
        P(None, "tm", None, None, None),
        P(),
        P(),
    )
    out_specs = P("op", None, "tm", None, None)
    return jax.shard_map(body, mesh=mesh, in_specs=in_specs, out_specs=out_specs, check_vma=False)
```

time: 413 us -> 178 us (0.43)
  waiting for transfers between devices: 176 us -> 0 us
  matrix products: 170 us -> 0 us
  Pallas kernels: 0 us -> 165 us
  local copies, waits for them, and re-layouts: 34.8 us -> 7.96 us
  between operations: 18.9 us -> 3.9 us
  other arithmetic: 9.7 us -> 0.19 us
    dot_general x12 -> x0, matrix products: 170 us -> none  [the longest x8 97.7 us: inner(): return jnp.einsum(spec, first, second, preferred_element_type=jnp.float32)]
    pallas_call x0 -> x1, Pallas kernels: none -> 165 us  [body(): pl.pallas_call(kernel, out_shape=jax.ShapeDtypeStruct((2, 2, 128, 256), F...]
    psum x1 -> x0, waiting for transfers between devices: 112 us -> none  [from_root(): return lax.psum(kept, axis)]
    all_gather x1 -> x0, waiting for transfers between devices: 63.4 us -> none  [body(): lax.all_gather(own_sources, 'op', axis=0, tiled=True)]
    unnamed x10 -> x0, local copies, waits for them, and re-layouts: 13.3 us -> none
    select_n x3 -> x0, other arithmetic: 6.57 us -> none  [the longest x2 4.03 us: body(): return jnp.take(mixed, partner, axis=4)]
    slice x3 -> x1, local copies, waits for them, and re-layouts: 7.53 us -> 1.34 us  [body(): src_times[s] % 8]
    gather x1 -> x0, local copies, waits for them, and re-layouts: 5.25 us -> none  [body(): return jnp.take(mixed, partner, axis=4)]
  transfers between devices with their start and end apart: 2 -> 0, of which waited for: 2 -> 0; matrix products, arithmetic and copies ran while one was open for 29% -> 0% of each run, Pallas kernels for 0% -> 0%
where the time goes in v1:
time: 178 us
  Pallas kernels  165 us (93%)
  local copies, waits for them, and re-layouts  7.96 us (4%)
  between operations  3.9 us (2%)
    pallas_call x1, Pallas kernels, body(): pl.pallas_call(kernel, out_shape=jax.ShapeDtypeStruct((2, 2, 128, 256), F...  165 us

profile of v1, /device:TPU:1, one launch (start us, length us, event | category | flops | bytes accessed | tf_op | source)
XLA Modules:
  0.0 177.5 jit_solution(2088362231008615128)
XLA Ops:
  0.0 1.3 fusion
  5.2 1.7 constant_dynamic-slice_fusion.1
  6.9 0.2 maximum_bitcast_fusion
  7.1 2.7 %copy.9 = bf16[4,2,2,16,2,16,128]{6,5,4,3,2,1,0:T(8,128)(2,1)} copy(bf16[4,2,2,16,2,16,128]{6,3,1,0,4,5,2:T(8,128)(2,1)S(1)} %maximum_bitcast_fusion) | data formatting | bytes 4194304 | tf_op jit(solution)/shard_map/transpose | solution.py:264
  9.8 165.4 %shard_map.55 = f32[2,2,128,256]{3,2,1,0:T(8,128)} custom-call(s32[2]{0:T(128)} %src.1, bf16[4,2,64,16,128]{4,3,2,1,0:T(8,128)(2,1)} %bitcast.16, bf16[16,8,2,128,128]{4,3,2,1,0:T(8,128)(2,1)} %phi.1, bf16[2,8,2,128,128]{4,3,2,1,0:T(8,128)(2,1)} %tauf.1, bf16[2,8,2,128,128]{4,3,2,1,0:T(8,128)(2,1)} %taub.1, s32[1,256]{1,0:T(1,128)} %bitcast.20), custom_call_target="tpu_custom_call" | custom-call | tf_op jit(solution)/shard_map/pallas_call | solution.py:266
  175.3 2.2 %copy.14 = f32[2,2,8,16,256]{4,1,2,0,3:T(2,128)} copy(f32[2,2,8,16,256]{4,3,2,1,0:T(8,128)} %bitcast.19) | data formatting | bytes 1048576 | tf_op jit(solution)/shard_map/reshape | solution.py:288

commit v2 on v1

--- a/solution.py
+++ b/solution.py
@@ -11,6 +11,7 @@
 F32 = jnp.float32
 BF16 = jnp.bfloat16
 NSEM = 136
+ROW = 132
 COLORS = ((0, 22, "xyz"), (22, 42, "yzx"), (42, 64, "zxy"))
 
 
@@ -18,8 +19,8 @@
     return lax.rem(v + step, 4)
 
 
-def kernel(src, cand, phi, tauf, taub, partner, out, S, P2, acc, stage, fbuf, fl, wb, rs, comb, dd,
-           send_sem, recv_sem, phi_sem):
+def kernel(src, phi, tauf_hbm, taub_hbm, partner, out, S, P2, acc, stage, abuf, fbuf, cand, tauf, taub, fl, wb, rs, comb, dd,
+           send_sem, recv_sem, phi_sem, tau_sem, load_sem):
     op = lax.axis_index("op")
     tm = lax.axis_index("tm")
     core = lax.rem(op, 2)
@@ -50,13 +51,38 @@
         slot = lax.rem(t, 2)
         return pltpu.make_async_copy(phi.at[:, t], fbuf.at[slot], phi_sem.at[slot])
 
-    phi_copy(0).start()
-
+    loads = [pltpu.make_async_copy(phi.at[j], P2.at[0, j * 8:j * 8 + 8], load_sem.at[j]) for j in range(16)]
+    for copy in loads:
+        copy.start()
     peers = [device({d: nxt(pos[d], k)}) for d in "xyz" for k in (1, 3)]
     peers += [device({"z": nxt(pos["z"], 2)}), device({}, True)]
     barrier = pltpu.get_barrier_semaphore()
     for peer in peers:
         pl.semaphore_signal(barrier, inc=1, device_id=peer, device_id_type=MESH)
+    taus = [pltpu.make_async_copy(tauf_hbm, tauf, tau_sem.at[0]), pltpu.make_async_copy(taub_hbm, taub, tau_sem.at[1])]
+    for copy in taus:
+        copy.start()
+    phi_copy(0).start()
+
+    for copy in loads:
+        copy.wait()
+    for s in range(2):
+        when = lax.rem(src[s], 8)
+        for j in range(16):
+            for r in range(2):
+                stage[r, j * ROW:j * ROW + 128, :] = P2[0, j * 8 + when, r].astype(F32)
+
+        def deal(ab, c2):
+            for q in range(8):
+                for r in range(2):
+                    rows = stage[r, pl.ds(ab * 8 + q, 16, stride=ROW), :]
+                    cand[ab // 4, lax.rem(ab // 2, 2), s * 32 + lax.rem(ab, 2) * 16 + q * 2 + r] = rows.astype(BF16)
+            return c2
+
+        lax.fori_loop(0, 16, deal, 0)
+    acc[...] = jnp.zeros_like(acc)
+    for copy in taus:
+        copy.wait()
     pl.semaphore_wait(barrier, len(peers))
 
     def sandwich(t, carry):
@@ -79,24 +105,22 @@
             wb[128:256, 0:128] = -bi
             wb[128:256, 128:256] = br
 
-            def pair(jp, c2):
+            for jp in range(8):
                 two = [fbuf[slot, 2 * jp + q].reshape(256, 128) for q in range(2)]
                 a = jnp.dot(fl[...], jnp.concatenate(two, axis=1), preferred_element_type=F32).astype(BF16)
                 for q in range(2):
-                    left = jnp.concatenate([a[0:128, q * 128:q * 128 + 128], a[128:256, q * 128:q * 128 + 128]], axis=1)
-                    prod = jnp.dot(left, wb[...], preferred_element_type=F32)
-                    row = pl.multiple_of((2 * jp + q) * 128, 128)
-                    stage[0, pl.ds(row, 128), :] = prod[:, 0:128]
-                    stage[1, pl.ds(row, 128), :] = prod[:, 128:256]
-                return c2
-
-            lax.fori_loop(0, 8, pair, 0)
+                    for r in range(2):
+                        abuf[(2 * jp + q) * 128:(2 * jp + q) * 128 + 128, r * 128:r * 128 + 128] = a[r * 128:r * 128 + 128, q * 128:q * 128 + 128]
+            for j in range(16):
+                prod = jnp.dot(abuf[j * 128:j * 128 + 128, :], wb[...], preferred_element_type=F32)
+                for r in range(2):
+                    stage[r, j * ROW:j * ROW + 128, :] = prod[:, r * 128:r * 128 + 128]
 
             def turn(ab, c2):
                 for q in range(8):
                     for r in range(2):
                         a = ab * 8 + q
-                        rows = stage[r, pl.ds(a, 16, stride=128), :]
+                        rows = stage[r, pl.ds(a, 16, stride=ROW), :]
                         P2[s, a, r, pl.ds(pl.multiple_of(t * 16, 16), 16), :] = rows.astype(BF16)
                 return c2
 
@@ -115,7 +139,7 @@
         send(cand.at[xp, 1], rs.at[2], plus),
         send(cand.at[xm, 0], rs.at[3], minus),
     ]
-    lax.fori_loop(0, 4, sandwich, 0)
+    lax.fori_loop(0, 3, sandwich, 0)
     first[0].wait_recv()
     first[1].wait_recv()
     for s in range(2):
@@ -123,7 +147,7 @@
         comb[0, h] = jnp.where(own_x[s] == xm, rs[0, h], cand[xp, 0, h])
         comb[1, h] = jnp.where(own_x[s] == xp, rs[1, h], cand[xm, 1, h])
     second = [send(comb.at[0], rs.at[4], plus), send(comb.at[1], rs.at[5], minus)]
-    lax.fori_loop(4, 6, sandwich, 0)
+    lax.fori_loop(3, 7, sandwich, 0)
     for copy in first[2:] + second:
         copy.wait_recv()
     for s in range(2):
@@ -131,7 +155,7 @@
         dd[0, h] = jnp.where(own_x[s] == x, cand[x, 0, h], jnp.where(own_x[s] == xp, rs[3, h], rs[4, h]))
         dd[1, h] = jnp.where(own_x[s] == x, cand[x, 1, h], jnp.where(own_x[s] == xm, rs[2, h], rs[5, h]))
     across = send(dd.at[1 - zh], rs.at[6], device({"z": nxt(pos["z"], 2)}))
-    lax.fori_loop(6, 8, sandwich, 0)
+    lax.fori_loop(7, 8, sandwich, 0)
     across.wait_recv()
     for s in range(2):
         h = slice(32 * s, 32 * s + 32)
@@ -147,11 +171,11 @@
         return pl.ds(v, 1)
 
     mate = device({}, True)
-    mate_copies = {0: [], 1: [], 2: []}
-
-    def share(color, where, lo, hi):
-        ref = box(where, lo, hi)
-        mate_copies[color].append(send(ref, ref, mate))
+    mate_copies = {(c, k): [] for c in range(3) for k in range(4)}
+
+    def share(color, k, where):
+        ref = box(where, *COLORS[color][:2])
+        mate_copies[color, k].append(send(ref, ref, mate))
 
     def ring1(color, d, where):
         lo, hi, _ = COLORS[color]
@@ -190,7 +214,7 @@
         line[c][order[c][0]] = whole
         p2[c] = ring1(c, order[c][1], line[c])
         p3[c][0] = ring1(c, order[c][2], line[c])
-        share(c, line[c], COLORS[c][0], COLORS[c][1])
+        share(c, 0, line[c])
 
     def group(c, k):
         w = dict(line[c])
@@ -202,53 +226,78 @@
         p2b[c] = ring2(c, order[c][1], line[c])
         for k in (1, 2):
             p3[c][k] = ring1(c, order[c][2], group(c, k))
-            share(c, group(c, k), COLORS[c][0], COLORS[c][1])
+            share(c, k, group(c, k))
     for c in three:
         arrived(p2b[c])
         p3[c][3] = ring1(c, order[c][2], group(c, 3))
-        share(c, group(c, 3), COLORS[c][0], COLORS[c][1])
-    for k in range(4):
+        share(c, 3, group(c, 3))
+    def forward(k):
         for c in three:
             arrived(p3[c][k])
             p3b[c][k] = ring2(c, order[c][2], group(c, k))
             for step in (3, 1):
                 w = group(c, k)
                 w[order[c][2]] = one(nxt(pos[order[c][2]], step))
-                share(c, w, COLORS[c][0], COLORS[c][1])
-    for k in range(4):
+                share(c, k, w)
+
+    def settle(k):
         for c in three:
             arrived(p3b[c][k])
             w = group(c, k)
             w[order[c][2]] = one(nxt(pos[order[c][2]], 2))
-            share(c, w, COLORS[c][0], COLORS[c][1])
-
-    acc[...] = jnp.zeros_like(acc)
-
-    def contract(s, a0, a1):
-        def step(p, c2):
-            xx = p // 2
-            z0 = lax.rem(p, 2) * 2
-            left, right = [], []
-            for a in range(a0, a1):
-                half = [S[xx, pl.ds(z0, 2), :, :, s * 32 + a * 2 + r].reshape(256, 128) for r in range(2)]
-                left.append(jnp.concatenate(half, axis=0))
-                right.append(P2[s, p * 16 + a].reshape(256, 128))
-            acc[s] += lax.dot_general(
-                jnp.concatenate(left, axis=1), jnp.concatenate(right, axis=1),
-                (((1,), (1,)), ((), ())), preferred_element_type=F32)
-            return c2
-
-        lax.fori_loop(0, 8, step, 0)
-
-    parts = {0: ((0, 0, 11),), 1: ((0, 11, 16), (1, 0, 5)), 2: ((1, 5, 16),)}
-    for c in three:
-        arrived(mate_copies[c])
-        for part in parts[c]:
-            contract(*part)
+            share(c, k, w)
+
+    def product(s, p, a0, a1, fields):
+        left, right = [], []
+        for a in range(a0, a1):
+            half = [fields(s * 32 + a * 2 + r) for r in range(2)]
+            left.append(jnp.concatenate(half, axis=0))
+            right.append(P2[s, p * 16 + a].reshape(256, 128))
+        return lax.dot_general(
+            jnp.concatenate(left, axis=1), jnp.concatenate(right, axis=1),
+            (((1,), (1,)), ((), ())), preferred_element_type=F32)
+
+    def contract(k):
+        for c in three:
+            arrived(mate_copies[c, k])
+            v = nxt(pos[order[c][1]], (0, 3, 1, 2)[k])
+            if c == 0:
+                def step(p, c2):
+                    got = product(0, p, 0, 11, lambda slab: S[
+                        p // 2, pl.ds(lax.rem(p, 2) * 2, 2), v, :, slab].reshape(64, 128))
+                    acc[0, :, :, v] += got.reshape(2, 2, 32, 256)
+                    return c2
+                lax.fori_loop(0, 8, step, 0)
+            elif c == 1:
+                def step(xx, c2):
+                    for s, a0, a1 in ((0, 11, 16), (1, 0, 5)):
+                        got = product(s, xx * 2 + v // 2, a0, a1, lambda slab: S[xx, v, :, :, slab].reshape(128, 128))
+                        acc[s, :, lax.rem(v, 2)] += got.reshape(2, 4, 32, 256)
+                    return c2
+                lax.fori_loop(0, 4, step, 0)
+            else:
+                def step(h, c2):
+                    got = product(1, v * 2 + h, 5, 16, lambda slab: S[v, pl.ds(h * 2, 2), :, :, slab].reshape(256, 128))
+                    acc[1] += got.reshape(2, 2, 4, 32, 256)
+                    return c2
+                lax.fori_loop(0, 2, step, 0)
+
+    forward(0)
+    forward(1)
+    settle(0)
+    forward(2)
+    contract(0)
+    settle(1)
+    forward(3)
+    contract(1)
+    settle(2)
+    settle(3)
+    contract(2)
+    contract(3)
 
     hot = (partner[...] == lax.broadcasted_iota(jnp.int32, (256, 256), 0)).astype(F32)
     for s in range(2):
-        q = acc[s]
+        q = acc[s].reshape(512, 256)
         real = q[0:256, 0:128] + q[256:512, 128:256]
         imag = q[0:256, 128:256] - q[256:512, 0:128]
         for r, v in enumerate((real, imag)):
@@ -260,20 +309,23 @@
 
 
 def body(phi, tau_fwd, tau_bwd, src_times, partner):
-    picked = jnp.stack([lax.dynamic_index_in_dim(phi, src_times[s] % 8, 1, False) for s in range(2)])
-    cand = picked.reshape(2, 16, 2, 4, 2, 16, 128).transpose(3, 4, 0, 5, 2, 1, 6).reshape(4, 2, 64, 16, 128)
     vm = pl.BlockSpec(memory_space=pltpu.VMEM)
+    hbm = pl.BlockSpec(memory_space=pl.ANY)
     res = pl.pallas_call(
         kernel,
         out_shape=jax.ShapeDtypeStruct((2, 2, 128, 256), F32),
-        in_specs=[pl.BlockSpec(memory_space=pltpu.SMEM), vm, pl.BlockSpec(memory_space=pl.ANY), vm, vm, vm],
+        in_specs=[pl.BlockSpec(memory_space=pltpu.SMEM), hbm, hbm, hbm, vm],
         out_specs=vm,
         scratch_shapes=[
             pltpu.VMEM((4, 4, 4, 2, 64, 16, 128), BF16),
             pltpu.VMEM((2, 128, 2, 128, 128), BF16),
-            pltpu.VMEM((2, 512, 256), F32),
-            pltpu.VMEM((2, 2048, 128), F32),
+            pltpu.VMEM((2, 2, 2, 4, 32, 256), F32),
+            pltpu.VMEM((2, 16 * ROW, 128), F32),
+            pltpu.VMEM((2048, 256), BF16),
             pltpu.VMEM((2, 16, 2, 128, 128), BF16),
+            pltpu.VMEM((4, 2, 64, 16, 128), BF16),
+            pltpu.VMEM((2, 8, 2, 128, 128), BF16),
+            pltpu.VMEM((2, 8, 2, 128, 128), BF16),
             pltpu.VMEM((256, 256), BF16),
             pltpu.VMEM((256, 256), BF16),
             pltpu.VMEM((7, 64, 16, 128), BF16),
@@ -282,9 +334,11 @@
             pltpu.SemaphoreType.DMA((NSEM,)),
             pltpu.SemaphoreType.DMA((NSEM,)),
             pltpu.SemaphoreType.DMA((2,)),
+            pltpu.SemaphoreType.DMA((2,)),
+            pltpu.SemaphoreType.DMA((16,)),
         ],
         compiler_params=pltpu.CompilerParams(collective_id=0, has_side_effects=True, vmem_limit_bytes=67043328),
-    )(src_times, cand, phi, tau_fwd, tau_bwd, partner.reshape(1, 256))
+    )(src_times, phi, tau_fwd, tau_bwd, partner.reshape(1, 256))
     return res.reshape(2, 2, 8, 16, 256).transpose(3, 0, 2, 1, 4)
 
 

time: 178 us -> 128 us (0.72)
  Pallas kernels: 165 us -> 125 us
  local copies, waits for them, and re-layouts: 7.96 us -> 2.24 us
  between operations: 3.9 us -> 0.01 us
    pallas_call x1, Pallas kernels: 165 us -> 125 us  [body(): pl.pallas_call(kernel, out_shape=jax.ShapeDtypeStruct((2, 2, 128, 256), F...]
    transpose x1 -> x0, local copies, waits for them, and re-layouts: 2.69 us -> none  [body(): picked.reshape(2, 16, 2, 4, 2, 16, 128).transpose(3, 4, 0, 5, 2, 1, 6)]
where the time goes in v2:
time: 128 us
  Pallas kernels  125 us (98%)
  local copies, waits for them, and re-layouts  2.24 us (2%)
    pallas_call x1, Pallas kernels, body(): pl.pallas_call(kernel, out_shape=jax.ShapeDtypeStruct((2, 2, 128, 256), F...  125 us

profile of v2, /device:TPU:1, one launch (start us, length us, event | category | flops | bytes accessed | tf_op | source)
XLA Modules:
  0.0 127.6 jit_solution(8134710898157948085)
XLA Ops:
  0.0 125.3 %shard_map.55 = f32[2,2,128,256]{3,2,1,0:T(8,128)} custom-call(s32[2]{0:T(128)} %src.1, bf16[16,8,2,128,128]{4,3,2,1,0:T(8,128)(2,1)} %phi.1, bf16[2,8,2,128,128]{4,3,2,1,0:T(8,128)(2,1)} %tauf_hbm.1, bf16[2,8,2,128,128]{4,3,2,1,0:T(8,128)(2,1)} %taub_hbm.1, s32[1,256]{1,0:T(1,128)} %bitcast.6), custom_call_target="tpu_custom_call" | custom-call | tf_op jit(solution)/shard_map/pallas_call | solution.py:314
  125.3 2.2 %copy.8 = f32[2,2,8,16,256]{4,1,2,0,3:T(2,128)} copy(f32[2,2,8,16,256]{4,3,2,1,0:T(8,128)} %bitcast.5) | data formatting | bytes 1048576 | tf_op jit(solution)/shard_map/reshape | solution.py:342

commit v3 on v2

--- a/solution.py
+++ b/solution.py
@@ -10,16 +10,21 @@
 MESH = pl.DeviceIdType.MESH
 F32 = jnp.float32
 BF16 = jnp.bfloat16
-NSEM = 136
+NSEM = 168
 ROW = 132
 COLORS = ((0, 22, "xyz"), (22, 42, "yzx"), (42, 64, "zxy"))
+PARTS = (((0, 0, 6), (1, 0, 5)), ((0, 6, 11), (1, 5, 10)), ((0, 11, 16), (1, 10, 16)))
+GROUPS = ((0, 0, 4), (3, 0, 4), (1, 0, 4), (2, 0, 2), (2, 2, 2))
+XF = 10
+ZF = 16 - XF
+ZH = ZF // 2
 
 
 def nxt(v, step):
     return lax.rem(v + step, 4)
 
 
-def kernel(src, phi, tauf_hbm, taub_hbm, partner, out, S, P2, acc, stage, abuf, fbuf, cand, tauf, taub, fl, wb, rs, comb, dd,
+def kernel(src, phi, tauf_hbm, taub_hbm, partner, out, S, P2, acc, stage, abuf, fbuf, cand, tauf, taub, fl, wb, rs, comb, dd, rz, rw, ee, rv, comb2,
            send_sem, recv_sem, phi_sem, tau_sem, load_sem):
     op = lax.axis_index("op")
     tm = lax.axis_index("tm")
@@ -76,7 +81,7 @@
             for q in range(8):
                 for r in range(2):
                     rows = stage[r, pl.ds(ab * 8 + q, 16, stride=ROW), :]
-                    cand[ab // 4, lax.rem(ab // 2, 2), s * 32 + lax.rem(ab, 2) * 16 + q * 2 + r] = rows.astype(BF16)
+                    cand[ab // 4, lax.rem(ab // 2, 2), lax.rem(ab, 2) * 8 + q, s * 2 + r] = rows.astype(BF16)
             return c2
 
         lax.fori_loop(0, 16, deal, 0)
@@ -133,33 +138,77 @@
     x = pos["x"]
     xp, xm, x2 = nxt(x, 1), nxt(x, 3), nxt(x, 2)
     plus, minus = device({"x": xp}), device({"x": xm})
+    far = device({"z": nxt(pos["z"], 2)})
+
+    def choose(s, picks, last):
+        value = last
+        for condition, other in reversed(picks):
+            value = jnp.where(condition[s], other, value)
+        return value
+
+    def pick(out_ref, pairs, last):
+        for s in range(2):
+            h = slice(2 * s, 2 * s + 2)
+            out_ref[:, h] = choose(s, [(c, r[:, h]) for c, r in pairs], last[:, h])
+
+    at_x = [v == x for v in own_x]
+    at_xp = [v == xp for v in own_x]
+    at_xm = [v == xm for v in own_x]
+    at_zh = [v == zh for v in own_zh]
+
+    early = pl.ds(0, XF)
+    late = pl.ds(XF, ZF)
+    pair1 = send(cand.at[:, 1 - zh, late], rz, far)
     first = [
-        send(cand.at[x2, 0], rs.at[0], plus),
-        send(cand.at[x2, 1], rs.at[1], minus),
-        send(cand.at[xp, 1], rs.at[2], plus),
-        send(cand.at[xm, 0], rs.at[3], minus),
+        send(cand.at[x2, 0, early], rs.at[0], plus),
+        send(cand.at[x2, 1, early], rs.at[1], minus),
+        send(cand.at[xp, 1, early], rs.at[2], plus),
+        send(cand.at[xm, 0, early], rs.at[3], minus),
     ]
-    lax.fori_loop(0, 3, sandwich, 0)
+    lax.fori_loop(0, 2, sandwich, 0)
     first[0].wait_recv()
     first[1].wait_recv()
-    for s in range(2):
-        h = slice(32 * s, 32 * s + 32)
-        comb[0, h] = jnp.where(own_x[s] == xm, rs[0, h], cand[xp, 0, h])
-        comb[1, h] = jnp.where(own_x[s] == xp, rs[1, h], cand[xm, 1, h])
+    pick(comb.at[0], [(at_xm, rs.at[0])], cand.at[xp, 0, early])
+    pick(comb.at[1], [(at_xp, rs.at[1])], cand.at[xm, 1, early])
     second = [send(comb.at[0], rs.at[4], plus), send(comb.at[1], rs.at[5], minus)]
-    lax.fori_loop(3, 7, sandwich, 0)
+    lax.fori_loop(2, 4, sandwich, 0)
+    pair1.wait_recv()
+    for q in range(4):
+        pick(ee.at[q], [(at_zh, cand.at[q, zh, late])], rz.at[q])
+    lo, hi = pl.ds(0, ZH), pl.ds(ZH, ZH)
+    third = [
+        send(ee.at[x2, lo], rv.at[0], plus),
+        send(ee.at[x2, hi], rv.at[1], minus),
+        send(ee.at[xp, hi], rv.at[2], plus),
+        send(ee.at[xm, lo], rv.at[3], minus),
+    ]
     for copy in first[2:] + second:
         copy.wait_recv()
-    for s in range(2):
-        h = slice(32 * s, 32 * s + 32)
-        dd[0, h] = jnp.where(own_x[s] == x, cand[x, 0, h], jnp.where(own_x[s] == xp, rs[3, h], rs[4, h]))
-        dd[1, h] = jnp.where(own_x[s] == x, cand[x, 1, h], jnp.where(own_x[s] == xm, rs[2, h], rs[5, h]))
-    across = send(dd.at[1 - zh], rs.at[6], device({"z": nxt(pos["z"], 2)}))
-    lax.fori_loop(7, 8, sandwich, 0)
-    across.wait_recv()
-    for s in range(2):
-        h = slice(32 * s, 32 * s + 32)
-        S[pos["x"], pos["z"], pos["y"], core, h] = jnp.where(own_zh[s] == zh, dd[zh, h], rs[6, h])
+    pick(dd.at[0], [(at_x, cand.at[x, 0, early]), (at_xp, rs.at[3])], rs.at[4])
+    pick(dd.at[1], [(at_x, cand.at[x, 1, early]), (at_xm, rs.at[2])], rs.at[5])
+    pair2 = send(dd.at[1 - zh], rw, far)
+    lax.fori_loop(4, 5, sandwich, 0)
+    third[0].wait_recv()
+    third[1].wait_recv()
+    pick(comb2.at[0], [(at_xm, rv.at[0])], ee.at[xp, lo])
+    pick(comb2.at[1], [(at_xp, rv.at[1])], ee.at[xm, hi])
+    fourth = [send(comb2.at[0], rv.at[4], plus), send(comb2.at[1], rv.at[5], minus)]
+    lax.fori_loop(5, 6, sandwich, 0)
+    own = S.at[pos["x"], pos["z"], pos["y"], core]
+    pair2.wait_recv()
+    for a in range(XF):
+        for s in range(2):
+            h = slice(2 * s, 2 * s + 2)
+            own[4 * a + 2 * s:4 * a + 2 * s + 2] = choose(s, [(at_zh, dd[zh, a, h])], rw[a, h])
+    for copy in third[2:] + fourth:
+        copy.wait_recv()
+    for half, mid, side, relay in ((0, at_xp, 3, 4), (1, at_xm, 2, 5)):
+        for b in range(ZH):
+            a = half * ZH + b
+            for s in range(2):
+                h = slice(2 * s, 2 * s + 2)
+                row = 4 * (XF + a) + 2 * s
+                own[row:row + 2] = choose(s, [(at_x, ee[x, a, h]), (mid, rv[side, b, h])], rv[relay, b, h])
 
     whole = pl.ds(0, 4)
 
@@ -171,7 +220,7 @@
         return pl.ds(v, 1)
 
     mate = device({}, True)
-    mate_copies = {(c, k): [] for c in range(3) for k in range(4)}
+    mate_copies = {(c, k): [] for c in range(3) for k in range(len(GROUPS))}
 
     def share(color, k, where):
         ref = box(where, *COLORS[color][:2])
@@ -203,8 +252,8 @@
     base = {d: one(pos[d]) for d in "xyz"}
     p1 = [ring1(c, order[c][0], base) for c in three]
     p1b, p2, p2b = [None] * 3, [None] * 3, [None] * 3
-    p3 = [[None] * 4 for _ in three]
-    p3b = [[None] * 4 for _ in three]
+    p3 = [[None] * len(GROUPS) for _ in three]
+    p3b = [[None] * len(GROUPS) for _ in three]
     for c in three:
         arrived(p1[c])
         p1b[c] = ring2(c, order[c][0], base)
@@ -213,24 +262,25 @@
         arrived(p1b[c])
         line[c][order[c][0]] = whole
         p2[c] = ring1(c, order[c][1], line[c])
-        p3[c][0] = ring1(c, order[c][2], line[c])
-        share(c, 0, line[c])
 
     def group(c, k):
+        step, first_place, places = GROUPS[k]
         w = dict(line[c])
-        w[order[c][1]] = one(nxt(pos[order[c][1]], (0, 3, 1, 2)[k]))
+        w[order[c][0]] = pl.ds(first_place, places)
+        w[order[c][1]] = one(nxt(pos[order[c][1]], step))
         return w
 
+    def spread(c, k):
+        p3[c][k] = ring1(c, order[c][2], group(c, k))
+        share(c, k, group(c, k))
+
+    for c in three:
+        spread(c, 0)
+    lax.fori_loop(6, 8, sandwich, 0)
     for c in three:
         arrived(p2[c])
         p2b[c] = ring2(c, order[c][1], line[c])
-        for k in (1, 2):
-            p3[c][k] = ring1(c, order[c][2], group(c, k))
-            share(c, k, group(c, k))
-    for c in three:
-        arrived(p2b[c])
-        p3[c][3] = ring1(c, order[c][2], group(c, 3))
-        share(c, 3, group(c, 3))
+
     def forward(k):
         for c in three:
             arrived(p3[c][k])
@@ -250,50 +300,71 @@
     def product(s, p, a0, a1, fields):
         left, right = [], []
         for a in range(a0, a1):
-            half = [fields(s * 32 + a * 2 + r) for r in range(2)]
+            half = [fields(a * 4 + s * 2 + r) for r in range(2)]
             left.append(jnp.concatenate(half, axis=0))
             right.append(P2[s, p * 16 + a].reshape(256, 128))
         return lax.dot_general(
             jnp.concatenate(left, axis=1), jnp.concatenate(right, axis=1),
             (((1,), (1,)), ((), ())), preferred_element_type=F32)
 
-    def contract(k):
+    def contract(c, k):
+        arrived(mate_copies[c, k])
+        off, first_place, places = GROUPS[k]
+        v = nxt(pos[order[c][1]], off)
+        if c == 0:
+            def step(p, c2):
+                got = [product(*part[:1], p, *part[1:], lambda slab: S[
+                    p // 2, pl.ds(lax.rem(p, 2) * 2, 2), v, :, slab].reshape(64, 128)) for part in PARTS[c]]
+                for s, value in enumerate(got):
+                    acc[s, :, :, v] += value.reshape(2, 2, 32, 256)
+                return c2
+            lax.fori_loop(2 * first_place, 2 * (first_place + places), step, 0, unroll=2)
+        elif c == 1:
+            ys = pl.ds(first_place, places)
+
+            def step(xx, c2):
+                got = [product(*part[:1], xx * 2 + v // 2, *part[1:], lambda slab: S[
+                    xx, v, ys, :, slab].reshape(places * 32, 128)) for part in PARTS[c]]
+                for s, value in enumerate(got):
+                    acc[s, :, lax.rem(v, 2), ys] += value.reshape(2, places, 32, 256)
+                return c2
+            lax.fori_loop(0, 4, step, 0, unroll=2)
+        else:
+            for h in range(first_place // 2, (first_place + places) // 2):
+                for part in PARTS[c]:
+                    got = product(*part[:1], v * 2 + h, *part[1:], lambda slab: S[
+                        v, 2 * h:2 * h + 2, :, :, slab].reshape(256, 128))
+                    acc[part[0]] += got.reshape(2, 2, 4, 32, 256)
+
+    def contract_all(k):
         for c in three:
-            arrived(mate_copies[c, k])
-            v = nxt(pos[order[c][1]], (0, 3, 1, 2)[k])
-            if c == 0:
-                def step(p, c2):
-                    got = product(0, p, 0, 11, lambda slab: S[
-                        p // 2, pl.ds(lax.rem(p, 2) * 2, 2), v, :, slab].reshape(64, 128))
-                    acc[0, :, :, v] += got.reshape(2, 2, 32, 256)
-                    return c2
-                lax.fori_loop(0, 8, step, 0)
-            elif c == 1:
-                def step(xx, c2):
-                    for s, a0, a1 in ((0, 11, 16), (1, 0, 5)):
-                        got = product(s, xx * 2 + v // 2, a0, a1, lambda slab: S[xx, v, :, :, slab].reshape(128, 128))
-                        acc[s, :, lax.rem(v, 2)] += got.reshape(2, 4, 32, 256)
-                    return c2
-                lax.fori_loop(0, 4, step, 0)
-            else:
-                def step(h, c2):
-                    got = product(1, v * 2 + h, 5, 16, lambda slab: S[v, pl.ds(h * 2, 2), :, :, slab].reshape(256, 128))
-                    acc[1] += got.reshape(2, 2, 4, 32, 256)
-                    return c2
-                lax.fori_loop(0, 2, step, 0)
+            contract(c, k)
+
+    def spread_all(k):
+        for c in three:
+            spread(c, k)
 
     forward(0)
+    spread_all(1)
+    spread_all(2)
+    for c in three:
+        arrived(p2b[c])
+    settle(0)
+    contract_all(0)
     forward(1)
-    settle(0)
+    spread_all(3)
     forward(2)
-    contract(0)
+    spread_all(4)
     settle(1)
+    contract_all(1)
     forward(3)
-    contract(1)
     settle(2)
+    forward(4)
+    contract_all(2)
     settle(3)
-    contract(2)
-    contract(3)
+    contract_all(3)
+    settle(4)
+    contract_all(4)
 
     hot = (partner[...] == lax.broadcasted_iota(jnp.int32, (256, 256), 0)).astype(F32)
     for s in range(2):
@@ -323,14 +394,19 @@
             pltpu.VMEM((2, 16 * ROW, 128), F32),
             pltpu.VMEM((2048, 256), BF16),
             pltpu.VMEM((2, 16, 2, 128, 128), BF16),
-            pltpu.VMEM((4, 2, 64, 16, 128), BF16),
+            pltpu.VMEM((4, 2, 16, 4, 16, 128), BF16),
             pltpu.VMEM((2, 8, 2, 128, 128), BF16),
             pltpu.VMEM((2, 8, 2, 128, 128), BF16),
             pltpu.VMEM((256, 256), BF16),
             pltpu.VMEM((256, 256), BF16),
-            pltpu.VMEM((7, 64, 16, 128), BF16),
-            pltpu.VMEM((2, 64, 16, 128), BF16),
-            pltpu.VMEM((2, 64, 16, 128), BF16),
+            pltpu.VMEM((6, XF, 4, 16, 128), BF16),
+            pltpu.VMEM((2, XF, 4, 16, 128), BF16),
+            pltpu.VMEM((2, XF, 4, 16, 128), BF16),
+            pltpu.VMEM((4, ZF, 4, 16, 128), BF16),
+            pltpu.VMEM((XF, 4, 16, 128), BF16),
+            pltpu.VMEM((4, ZF, 4, 16, 128), BF16),
+            pltpu.VMEM((6, ZH, 4, 16, 128), BF16),
+            pltpu.VMEM((2, ZH, 4, 16, 128), BF16),
             pltpu.SemaphoreType.DMA((NSEM,)),
             pltpu.SemaphoreType.DMA((NSEM,)),
             pltpu.SemaphoreType.DMA((2,)),

time: 128 us -> 111 us (0.87)
  Pallas kernels: 125 us -> 108 us
    pallas_call x1, Pallas kernels: 125 us -> 108 us  [body(): pl.pallas_call(kernel, out_shape=jax.ShapeDtypeStruct((2, 2, 128, 256), F...]
where the time goes in v3:
time: 111 us; the launch traced here: 110 us
  Pallas kernels  108 us (97%)
  local copies, waits for them, and re-layouts  2.24 us (2%)
    pallas_call x1, Pallas kernels, body(): pl.pallas_call(kernel, out_shape=jax.ShapeDtypeStruct((2, 2, 128, 256), F...  108 us
    reshape x1, local copies, waits for them, and re-layouts, body(): return res.reshape(2, 2, 8, 16, 256).transpose(3, 0, 2, 1, 4)  2.24 us

profile of v3, /device:TPU:1, one launch (start us, length us, event | category | flops | bytes accessed | tf_op | source)
XLA Modules:
  0.0 110.3 jit_solution(1841098556594341946)
XLA Ops:
  0.0 108.1 %shard_map.55 = f32[2,2,128,256]{3,2,1,0:T(8,128)} custom-call(s32[2]{0:T(128)} %src.1, bf16[16,8,2,128,128]{4,3,2,1,0:T(8,128)(2,1)} %phi.1, bf16[2,8,2,128,128]{4,3,2,1,0:T(8,128)(2,1)} %tauf_hbm.1, bf16[2,8,2,128,128]{4,3,2,1,0:T(8,128)(2,1)} %taub_hbm.1, s32[1,256]{1,0:T(1,128)} %bitcast.6), custom_call_target="tpu_custom_call" | custom-call | tf_op jit(solution)/shard_map/pallas_call | solution.py:385
  108.1 2.2 %copy.8 = f32[2,2,8,16,256]{4,1,2,0,3:T(2,128)} copy(f32[2,2,8,16,256]{4,3,2,1,0:T(8,128)} %bitcast.5) | data formatting | bytes 1048576 | tf_op jit(solution)/shard_map/reshape | solution.py:418

commit v4 on v3

--- a/solution.py
+++ b/solution.py
@@ -10,7 +10,7 @@
 MESH = pl.DeviceIdType.MESH
 F32 = jnp.float32
 BF16 = jnp.bfloat16
-NSEM = 168
+NSEM = 208
 ROW = 132
 COLORS = ((0, 22, "xyz"), (22, 42, "yzx"), (42, 64, "zxy"))
 PARTS = (((0, 0, 6), (1, 0, 5)), ((0, 6, 11), (1, 5, 10)), ((0, 11, 16), (1, 10, 16)))
@@ -200,6 +200,70 @@
         for s in range(2):
             h = slice(2 * s, 2 * s + 2)
             own[4 * a + 2 * s:4 * a + 2 * s + 2] = choose(s, [(at_zh, dd[zh, a, h])], rw[a, h])
+
+    whole = pl.ds(0, 4)
+
+    def box(where, lo, hi):
+        at = [where[d] for d in "xzy"]
+        return S.at[at[0], at[1], at[2], pl.ds(core, 1), pl.ds(lo, hi - lo)]
+
+    def one(v):
+        return pl.ds(v, 1)
+
+    mate = device({}, True)
+    mate_copies = {(c, k): [] for c in range(3) for k in range(len(GROUPS))}
+
+    def share(color, k, where):
+        ref = box(where, *COLORS[color][:2])
+        mate_copies[color, k].append(send(ref, ref, mate))
+
+    def ring1(color, d, where):
+        lo, hi, _ = COLORS[color]
+        w = dict(where)
+        w[d] = one(pos[d])
+        ref = box(w, lo, hi)
+        return [send(ref, ref, device({d: nxt(pos[d], k)})) for k in (1, 3)]
+
+    def ring2(color, d, where):
+        lo, hi, _ = COLORS[color]
+        mid = (lo + hi) // 2
+        w = dict(where)
+        w[d] = one(nxt(pos[d], 3))
+        a = box(w, lo, mid)
+        w[d] = one(nxt(pos[d], 1))
+        b = box(w, mid, hi)
+        return [send(a, a, device({d: nxt(pos[d], 1)})), send(b, b, device({d: nxt(pos[d], 3)}))]
+
+    def arrived(copies):
+        for copy in copies:
+            copy.wait_recv()
+
+    three = range(3)
+    order = [COLORS[c][2] for c in three]
+    base = {d: one(pos[d]) for d in "xyz"}
+    p1, p1b, p2, p2b = [None] * 3, [None] * 3, [[] for _ in three], [None] * 3
+    p3 = [[[] for _ in GROUPS] for _ in three]
+    p3b = [[None] * len(GROUPS) for _ in three]
+    line = [dict(base) for _ in three]
+    for c in three:
+        line[c][order[c][0]] = whole
+
+    def unit(c, u):
+        w = dict(base)
+        w[order[c][0]] = one(nxt(pos[order[c][0]], u))
+        return w
+
+    def second_ring(c, *units):
+        for u in units:
+            p2[c] += ring1(c, order[c][1], unit(c, u))
+
+    def third_ring(c, *units):
+        for u in units:
+            p3[c][0] += ring1(c, order[c][2], unit(c, u))
+
+    p1[0] = ring1(0, order[0][0], base)
+    second_ring(0, 0)
+    third_ring(0, 0)
     for copy in third[2:] + fourth:
         copy.wait_recv()
     for half, mid, side, relay in ((0, at_xp, 3, 4), (1, at_xm, 2, 5)):
@@ -209,59 +273,24 @@
                 h = slice(2 * s, 2 * s + 2)
                 row = 4 * (XF + a) + 2 * s
                 own[row:row + 2] = choose(s, [(at_x, ee[x, a, h]), (mid, rv[side, b, h])], rv[relay, b, h])
-
-    whole = pl.ds(0, 4)
-
-    def box(where, lo, hi):
-        at = [where[d] for d in "xzy"]
-        return S.at[at[0], at[1], at[2], pl.ds(core, 1), pl.ds(lo, hi - lo)]
-
-    def one(v):
-        return pl.ds(v, 1)
-
-    mate = device({}, True)
-    mate_copies = {(c, k): [] for c in range(3) for k in range(len(GROUPS))}
-
-    def share(color, k, where):
-        ref = box(where, *COLORS[color][:2])
-        mate_copies[color, k].append(send(ref, ref, mate))
-
-    def ring1(color, d, where):
-        lo, hi, _ = COLORS[color]
-        w = dict(where)
-        w[d] = one(pos[d])
-        ref = box(w, lo, hi)
-        return [send(ref, ref, device({d: nxt(pos[d], k)})) for k in (1, 3)]
-
-    def ring2(color, d, where):
-        lo, hi, _ = COLORS[color]
-        mid = (lo + hi) // 2
-        w = dict(where)
-        w[d] = one(nxt(pos[d], 3))
-        a = box(w, lo, mid)
-        w[d] = one(nxt(pos[d], 1))
-        b = box(w, mid, hi)
-        return [send(a, a, device({d: nxt(pos[d], 1)})), send(b, b, device({d: nxt(pos[d], 3)}))]
-
-    def arrived(copies):
-        for copy in copies:
-            copy.wait_recv()
-
-    three = range(3)
-    order = [COLORS[c][2] for c in three]
-    base = {d: one(pos[d]) for d in "xyz"}
-    p1 = [ring1(c, order[c][0], base) for c in three]
-    p1b, p2, p2b = [None] * 3, [None] * 3, [None] * 3
-    p3 = [[None] * len(GROUPS) for _ in three]
-    p3b = [[None] * len(GROUPS) for _ in three]
+    for c in (1, 2):
+        p1[c] = ring1(c, order[c][0], base)
+    for c in (1, 2):
+        second_ring(c, 0)
+    for c in (1, 2):
+        third_ring(c, 0)
+    lax.fori_loop(6, 7, sandwich, 0)
     for c in three:
         arrived(p1[c])
         p1b[c] = ring2(c, order[c][0], base)
-    line = [dict(base) for _ in three]
+    for c in three:
+        second_ring(c, 3, 1)
     for c in three:
         arrived(p1b[c])
-        line[c][order[c][0]] = whole
-        p2[c] = ring1(c, order[c][1], line[c])
+        second_ring(c, 2)
+    for c in three:
+        third_ring(c, 3, 1, 2)
+        share(c, 0, line[c])
 
     def group(c, k):
         step, first_place, places = GROUPS[k]
@@ -274,9 +303,7 @@
         p3[c][k] = ring1(c, order[c][2], group(c, k))
         share(c, k, group(c, k))
 
-    for c in three:
-        spread(c, 0)
-    lax.fori_loop(6, 8, sandwich, 0)
+    lax.fori_loop(7, 8, sandwich, 0)
     for c in three:
         arrived(p2[c])
         p2b[c] = ring2(c, order[c][1], line[c])

time: 111 us -> 108 us (0.973)
  Pallas kernels: 108 us -> 105 us
    pallas_call x1, Pallas kernels: 108 us -> 105 us  [body(): pl.pallas_call(kernel, out_shape=jax.ShapeDtypeStruct((2, 2, 128, 256), F...]
where the time goes in v4:
time: 108 us
  Pallas kernels  105 us (97%)
  local copies, waits for them, and re-layouts  2.24 us (2%)
    pallas_call x1, Pallas kernels, body(): pl.pallas_call(kernel, out_shape=jax.ShapeDtypeStruct((2, 2, 128, 256), F...  105 us
    reshape x1, local copies, waits for them, and re-layouts, body(): return res.reshape(2, 2, 8, 16, 256).transpose(3, 0, 2, 1, 4)  2.24 us

profile of v4, /device:TPU:1, one launch (start us, length us, event | category | flops | bytes accessed | tf_op | source)
XLA Modules:
  0.0 107.5 jit_solution(437584106699613654)
XLA Ops:
  0.0 105.3 %shard_map.55 = f32[2,2,128,256]{3,2,1,0:T(8,128)} custom-call(s32[2]{0:T(128)} %src.1, bf16[16,8,2,128,128]{4,3,2,1,0:T(8,128)(2,1)} %phi.1, bf16[2,8,2,128,128]{4,3,2,1,0:T(8,128)(2,1)} %tauf_hbm.1, bf16[2,8,2,128,128]{4,3,2,1,0:T(8,128)(2,1)} %taub_hbm.1, s32[1,256]{1,0:T(1,128)} %bitcast.6), custom_call_target="tpu_custom_call" | custom-call | tf_op jit(solution)/shard_map/pallas_call | solution.py:412
  105.3 2.2 %copy.8 = f32[2,2,8,16,256]{4,1,2,0,3:T(2,128)} copy(f32[2,2,8,16,256]{4,3,2,1,0:T(8,128)} %bitcast.5) | data formatting | bytes 1048576 | tf_op jit(solution)/shard_map/reshape | solution.py:445

commit v5 on v4

--- a/solution.py
+++ b/solution.py
@@ -334,38 +334,44 @@
             jnp.concatenate(left, axis=1), jnp.concatenate(right, axis=1),
             (((1,), (1,)), ((), ())), preferred_element_type=F32)
 
-    def contract(c, k):
-        arrived(mate_copies[c, k])
+    def contract(c, k, base_off, n_off, copies):
+        arrived(copies)
         off, first_place, places = GROUPS[k]
         v = nxt(pos[order[c][1]], off)
         if c == 0:
-            def step(p, c2):
-                got = [product(*part[:1], p, *part[1:], lambda slab: S[
-                    p // 2, pl.ds(lax.rem(p, 2) * 2, 2), v, :, slab].reshape(64, 128)) for part in PARTS[c]]
+            def step(i, c2):
+                z = nxt(pos["z"], base_off + i // places)
+                xx = first_place + lax.rem(i, places)
+                got = [product(*part[:1], xx * 2 + z // 2, *part[1:], lambda slab: S[
+                    xx, z, v, :, slab].reshape(32, 128)) for part in PARTS[c]]
                 for s, value in enumerate(got):
-                    acc[s, :, :, v] += value.reshape(2, 2, 32, 256)
+                    acc[s, :, lax.rem(z, 2), v] += value.reshape(2, 32, 256)
                 return c2
-            lax.fori_loop(2 * first_place, 2 * (first_place + places), step, 0, unroll=2)
+            lax.fori_loop(0, n_off * places, step, 0, unroll=2)
         elif c == 1:
             ys = pl.ds(first_place, places)
-
-            def step(xx, c2):
+            for i in range(n_off):
+                xx = nxt(pos["x"], base_off + i)
                 got = [product(*part[:1], xx * 2 + v // 2, *part[1:], lambda slab: S[
                     xx, v, ys, :, slab].reshape(places * 32, 128)) for part in PARTS[c]]
                 for s, value in enumerate(got):
                     acc[s, :, lax.rem(v, 2), ys] += value.reshape(2, places, 32, 256)
-                return c2
-            lax.fori_loop(0, 4, step, 0, unroll=2)
         else:
-            for h in range(first_place // 2, (first_place + places) // 2):
-                for part in PARTS[c]:
-                    got = product(*part[:1], v * 2 + h, *part[1:], lambda slab: S[
-                        v, 2 * h:2 * h + 2, :, :, slab].reshape(256, 128))
-                    acc[part[0]] += got.reshape(2, 2, 4, 32, 256)
-
-    def contract_all(k):
+            for i in range(n_off):
+                y = nxt(pos["y"], base_off + i)
+                for half in range(first_place // 2, (first_place + places) // 2):
+                    got = [product(*part[:1], v * 2 + half, *part[1:], lambda slab: S[
+                        v, 2 * half:2 * half + 2, y, :, slab].reshape(64, 128)) for part in PARTS[c]]
+                    for s, value in enumerate(got):
+                        acc[s, :, :, y] += value.reshape(2, 2, 32, 256)
+
+    def early(k):
         for c in three:
-            contract(c, k)
+            contract(c, k, 3, 3, mate_copies[c, k][:3])
+
+    def late(k):
+        for c in three:
+            contract(c, k, 2, 1, mate_copies[c, k][3:])
 
     def spread_all(k):
         for c in three:
@@ -376,22 +382,27 @@
     spread_all(2)
     for c in three:
         arrived(p2b[c])
+    early(0)
     settle(0)
-    contract_all(0)
+    late(0)
     forward(1)
     spread_all(3)
+    early(1)
     forward(2)
     spread_all(4)
     settle(1)
-    contract_all(1)
+    early(2)
     forward(3)
+    late(1)
     settle(2)
+    early(3)
+    late(2)
     forward(4)
-    contract_all(2)
     settle(3)
-    contract_all(3)
+    early(4)
     settle(4)
-    contract_all(4)
+    late(3)
+    late(4)
 
     hot = (partner[...] == lax.broadcasted_iota(jnp.int32, (256, 256), 0)).astype(F32)
     for s in range(2):

time: 108 us -> 107 us (level)
    pallas_call x1, Pallas kernels: 105 us -> 104 us  [body(): pl.pallas_call(kernel, out_shape=jax.ShapeDtypeStruct((2, 2, 128, 256), F...]
where the time goes in v5:
time: 107 us; the launch traced here: 106 us
  Pallas kernels  104 us (97%)
  local copies, waits for them, and re-layouts  2.24 us (2%)
    pallas_call x1, Pallas kernels, body(): pl.pallas_call(kernel, out_shape=jax.ShapeDtypeStruct((2, 2, 128, 256), F...  104 us
    reshape x1, local copies, waits for them, and re-layouts, body(): return res.reshape(2, 2, 8, 16, 256).transpose(3, 0, 2, 1, 4)  2.24 us

profile of v5, /device:TPU:1, one launch (start us, length us, event | category | flops | bytes accessed | tf_op | source)
XLA Modules:
  0.0 106.4 jit_solution(11160582711302691605)
XLA Ops:
  0.0 104.2 %shard_map.55 = f32[2,2,128,256]{3,2,1,0:T(8,128)} custom-call(s32[2]{0:T(128)} %src.1, bf16[16,8,2,128,128]{4,3,2,1,0:T(8,128)(2,1)} %phi.1, bf16[2,8,2,128,128]{4,3,2,1,0:T(8,128)(2,1)} %tauf_hbm.1, bf16[2,8,2,128,128]{4,3,2,1,0:T(8,128)(2,1)} %taub_hbm.1, s32[1,256]{1,0:T(1,128)} %bitcast.6), custom_call_target="tpu_custom_call" | custom-call | tf_op jit(solution)/shard_map/pallas_call | solution.py:423
  104.2 2.2 %copy.8 = f32[2,2,8,16,256]{4,1,2,0,3:T(2,128)} copy(f32[2,2,8,16,256]{4,3,2,1,0:T(8,128)} %bitcast.5) | data formatting | bytes 1048576 | tf_op jit(solution)/shard_map/reshape | solution.py:456

commit v6 on v5

--- a/solution.py
+++ b/solution.py
@@ -65,12 +65,12 @@
     for peer in peers:
         pl.semaphore_signal(barrier, inc=1, device_id=peer, device_id_type=MESH)
     taus = [pltpu.make_async_copy(tauf_hbm, tauf, tau_sem.at[0]), pltpu.make_async_copy(taub_hbm, taub, tau_sem.at[1])]
+
+    for copy in loads:
+        copy.wait()
     for copy in taus:
         copy.start()
     phi_copy(0).start()
-
-    for copy in loads:
-        copy.wait()
     for s in range(2):
         when = lax.rem(src[s], 8)
         for j in range(16):
@@ -84,10 +84,7 @@
                     cand[ab // 4, lax.rem(ab // 2, 2), lax.rem(ab, 2) * 8 + q, s * 2 + r] = rows.astype(BF16)
             return c2
 
-        lax.fori_loop(0, 16, deal, 0)
-    acc[...] = jnp.zeros_like(acc)
-    for copy in taus:
-        copy.wait()
+        lax.fori_loop(0, 16, deal, 0, unroll=4)
     pl.semaphore_wait(barrier, len(peers))
 
     def sandwich(t, carry):
@@ -165,6 +162,9 @@
         send(cand.at[xp, 1, early], rs.at[2], plus),
         send(cand.at[xm, 0, early], rs.at[3], minus),
     ]
+    acc[...] = jnp.zeros_like(acc)
+    for copy in taus:
+        copy.wait()
     lax.fori_loop(0, 2, sandwich, 0)
     first[0].wait_recv()
     first[1].wait_recv()

time: 107 us -> 106 us (level)
  no operation moved by 1% of the time
where the time goes in v6:
time: 106 us
  Pallas kernels  104 us (98%)
  local copies, waits for them, and re-layouts  2.24 us (2%)
    pallas_call x1, Pallas kernels, body(): pl.pallas_call(kernel, out_shape=jax.ShapeDtypeStruct((2, 2, 128, 256), F...  104 us
    reshape x1, local copies, waits for them, and re-layouts, body(): return res.reshape(2, 2, 8, 16, 256).transpose(3, 0, 2, 1, 4)  2.24 us

profile of v6, /device:TPU:1, one launch (start us, length us, event | category | flops | bytes accessed | tf_op | source)
XLA Modules:
  0.0 106.2 jit_solution(16000694059731538335)
XLA Ops:
  0.0 103.9 %shard_map.55 = f32[2,2,128,256]{3,2,1,0:T(8,128)} custom-call(s32[2]{0:T(128)} %src.1, bf16[16,8,2,128,128]{4,3,2,1,0:T(8,128)(2,1)} %phi.1, bf16[2,8,2,128,128]{4,3,2,1,0:T(8,128)(2,1)} %tauf_hbm.1, bf16[2,8,2,128,128]{4,3,2,1,0:T(8,128)(2,1)} %taub_hbm.1, s32[1,256]{1,0:T(1,128)} %bitcast.6), custom_call_target="tpu_custom_call" | custom-call | tf_op jit(solution)/shard_map/pallas_call | solution.py:423
  104.0 2.2 %copy.8 = f32[2,2,8,16,256]{4,1,2,0,3:T(2,128)} copy(f32[2,2,8,16,256]{4,3,2,1,0:T(8,128)} %bitcast.5) | data formatting | bytes 1048576 | tf_op jit(solution)/shard_map/reshape | solution.py:456
